TPU v7x, 256 devices: a whole 4x4x8 slice. The times are simulated.
256 devices in a mesh: stream: 32 (over y_hi, z, core), tm: 8 (over x, y_lo).
Axes of the slice: x: 4, y: 4 (y_hi: 2, y_lo: 2; y = y_hi * 2 + y_lo), z: 8, core: 2. Of those that a mesh axis runs over, the one named last changes fastest.
Arguments:
- signal: bfloat16 [64, 2, 4194304], P('stream', None, 'tm'), parts along dimension 0, may hold values from -11 to 11
- taps: float32 [16, 4096], replicated, may hold values from -1.5 to 1.5
Outputs:
- channels_out: float32 [64, 2, 4096, 1024], P('stream', None, 'tm'), parts along dimension 0
There are 32 independent parts, one for each index of `stream`. A program takes and returns all parts, laid end to end along the dimension named above; an argument that names none is the same for every part. Nothing has to cross between parts.
All inputs are finite; a program needn't handle non-finite values.
Results may differ from a plain program's by a relative error of at most 0.0003.
Values may be sent and summed in bfloat16 or wider, within the bound.
A program may use at most 128 MiB of HBM per device.

v0:
```python
import math

import jax
import jax.numpy as jnp
import numpy as np
from jax import lax
from jax.experimental import pallas as pl
from jax.experimental.pallas import tpu as pltpu
from jax.sharding import PartitionSpec as P

MESH = pl.DeviceIdType.MESH
F32 = jnp.float32
BF16 = jnp.bfloat16

LANES = 128
FIRST = 32
HALF = 16
TAPS_PITCH = 72
FRAME_PITCH = 72
CHANNEL_PITCH = 24
SPAN = 125.0
PEERS = ((2, 1), (2, 0), (1, 1), (3, 1), (0, 1), (1, 0), (3, 0))


def section_table():
    index = np.arange(LANES)
    angle = 2.0 * math.pi * (np.outer(index, index) % LANES) / LANES
    cos, sin = np.cos(angle) / 64.0, np.sin(angle) / 64.0
    return np.block([[cos, sin], [-sin, cos]]).astype(np.float32)


def twist_tables():
    angle = 2.0 * math.pi * np.outer(np.arange(FIRST), np.arange(LANES)) / (FIRST * LANES)
    return np.cos(angle).astype(np.float32), np.sin(angle).astype(np.float32)


def plus(a, b):
    return a[0] + b[0], a[1] + b[1]


def minus(a, b):
    return a[0] - b[0], a[1] - b[1]


def minus_i(a):
    return a[1], -a[0]


def turned(a, step, points):
    step %= points
    if step == 0:
        return a
    if step * 4 == points:
        return a[1], -a[0]
    if step * 2 == points:
        return -a[0], -a[1]
    if step * 8 == points:
        c = np.float32(math.sqrt(0.5))
        return (a[0] + a[1]) * c, (a[1] - a[0]) * c
    if step * 8 == 3 * points:
        c = np.float32(math.sqrt(0.5))
        return (a[1] - a[0]) * c, (a[0] + a[1]) * -c
    c = np.float32(math.cos(2.0 * math.pi * step / points))
    s = np.float32(math.sin(2.0 * math.pi * step / points))
    return a[0] * c + a[1] * s, a[1] * c - a[0] * s


def four(v):
    a, b = plus(v[0], v[2]), minus(v[0], v[2])
    c, d = plus(v[1], v[3]), minus_i(minus(v[1], v[3]))
    return [plus(a, c), plus(b, d), minus(a, c), minus(b, d)]


def eight(v):
    even, odd = four(v[0::2]), four(v[1::2])
    odd = [turned(odd[i], i, 8) for i in range(4)]
    return [plus(even[i], odd[i]) for i in range(4)] + [minus(even[i], odd[i]) for i in range(4)]


def first_section(load):
    parts = [[None] * 8 for _ in range(4)]
    for b in range(8):
        column = four([load(8 * a + b) for a in range(4)])
        for p in range(4):
            parts[p][b] = turned(column[p], b * p, FIRST)
    out = [None] * FIRST
    for p in range(4):
        for q, value in enumerate(eight(parts[p])):
            out[p + 4 * q] = value
    return out


def transposed_dot(a, b):
    return lax.dot_general(a, b, (((1,), (1,)), ((), ())), preferred_element_type=F32)


def channelize(streams, frames, ways, z_ref, taps_ref, high_ref, low_ref, cos_ref, sin_ref, got_ref, scales_ref,
               x_ref, taps_scr, frame_scr, grid_scr, channel_scr, send_ref, table_scr, table_ref,
               load_sem, halo_send, halo_recv, send_sem, recv_sem, table_send, table_recv, own_sem, own_table_sem):
    rows = 2 * FIRST
    halo = 16 * rows
    edge = 15 * rows
    own = LANES // ways
    me = lax.axis_index("tm")
    across, along = me // 2, lax.rem(me, 2)

    def peer_of(number):
        dx, dy = PEERS[number]
        return lax.rem(across + dx, ways // 2) * 2 + lax.rem(along + dy, 2)

    barrier = pltpu.get_barrier_semaphore()
    for number in range(ways - 1):
        pl.semaphore_signal(barrier, inc=1, device_id={"tm": peer_of(number)}, device_id_type=MESH)

    def load(s):
        return pltpu.make_async_copy(z_ref.at[s], x_ref.at[s, pl.ds(halo, frames * rows), :], load_sem.at[s])

    def pass_on(s):
        return pltpu.make_async_remote_copy(
            src_ref=z_ref.at[s, pl.ds(frames * rows - edge, edge), :],
            dst_ref=x_ref.at[s, pl.ds(halo - edge, edge), :],
            send_sem=halo_send.at[s],
            recv_sem=halo_recv.at[s],
            device_id={"tm": lax.rem(me + 1, ways)},
            device_id_type=MESH,
        )

    for s in range(streams):
        load(s).start()
    pl.semaphore_wait(barrier, ways - 1)

    @pl.when(me < ways - 1)
    def _():
        for s in range(streams):
            pass_on(s).start()

    @pl.when(me == 0)
    def _():
        for s in range(streams):
            x_ref[s, pl.ds(halo - edge, edge), :] = jnp.zeros((edge, LANES), BF16)

    for octet in range(2):
        for m1 in range(FIRST):
            block = taps_ref[pl.ds(8 * octet, 8), pl.ds(LANES * m1, LANES)]
            for part in range(2):
                taps_scr[pl.ds(8 * octet * TAPS_PITCH + 2 * m1 + part, 8, stride=TAPS_PITCH), :] = block

    lane = lax.broadcasted_iota(jnp.int32, (LANES, LANES), 1)

    def transform(s, tb):
        for g in range(rows // 16):
            total = [None] * 8
            for j in range(23):
                start = pl.multiple_of((8 * tb + 1 + j) * rows + 16 * g, 16)
                x = x_ref[s, pl.ds(start, 16), :].astype(F32)
                for o in range(8):
                    k = o + 15 - j
                    if 0 <= k < 16:
                        term = taps_scr[k * TAPS_PITCH + 16 * g : k * TAPS_PITCH + 16 * g + 16, :] * x
                        total[o] = term if total[o] is None else total[o] + term
            for o in range(8):
                frame_scr[o * FRAME_PITCH + 16 * g : o * FRAME_PITCH + 16 * g + 16, :] = total[o]

        def fetch(m1):
            return tuple(frame_scr[pl.ds(2 * m1 + part, 8, stride=FRAME_PITCH), :] for part in range(2))

        at = pl.ds(pl.multiple_of(8 * tb, 8), 8)
        for c1, (real, imag) in enumerate(first_section(fetch)):
            cos, sin = cos_ref[c1 : c1 + 1, :], sin_ref[c1 : c1 + 1, :]
            grid_scr[c1, at, 0:LANES] = real * cos + imag * sin
            grid_scr[c1, at, LANES : 2 * LANES] = imag * cos - real * sin

    def outgoing(s, h, number):
        peer = peer_of(number)
        return pltpu.make_async_remote_copy(
            src_ref=send_ref.at[s, h, peer],
            dst_ref=got_ref.at[s, h, me],
            send_sem=send_sem.at[s, h, number],
            recv_sem=recv_sem.at[s, h, me],
            device_id={"tm": peer},
            device_id_type=MESH,
        )

    def outgoing_table(s, number):
        peer = peer_of(number)
        return pltpu.make_async_remote_copy(
            src_ref=table_ref.at[s, pl.ds(pl.multiple_of(peer * own, own), own), :],
            dst_ref=scales_ref.at[s, me],
            send_sem=table_send.at[s, number],
            recv_sem=table_recv.at[s, me],
            device_id={"tm": peer},
            device_id_type=MESH,
        )

    def own_block(s, h):
        return pltpu.make_async_copy(send_ref.at[s, h, me], got_ref.at[s, h, me], own_sem.at[s, h])

    def own_table(s):
        return pltpu.make_async_copy(
            table_ref.at[s, pl.ds(pl.multiple_of(me * own, own), own), :], scales_ref.at[s, me], own_table_sem.at[s]
        )

    def incoming(s, h, number):
        peer = peer_of(number)
        return pltpu.make_async_remote_copy(
            src_ref=send_ref.at[s, h, peer],
            dst_ref=got_ref.at[s, h, peer],
            send_sem=send_sem.at[s, h, number],
            recv_sem=recv_sem.at[s, h, peer],
            device_id={"tm": peer},
            device_id_type=MESH,
        )

    def incoming_table(s, number):
        peer = peer_of(number)
        return pltpu.make_async_remote_copy(
            src_ref=table_ref.at[s, pl.ds(pl.multiple_of(peer * own, own), own), :],
            dst_ref=scales_ref.at[s, peer],
            send_sem=table_send.at[s, number],
            recv_sem=table_recv.at[s, peer],
            device_id={"tm": peer},
            device_id_type=MESH,
        )

    def second_section(h, place):
        c1 = h * HALF + place
        y = grid_scr[c1]
        high = y.astype(BF16)
        low = (y - high.astype(F32)).astype(BF16)
        wide = transposed_dot(high_ref[...], jnp.concatenate([high, low], axis=0))
        value = wide[:, :LANES] + wide[:, LANES:] + transposed_dot(low_ref[...], high)
        real, imag = value[:LANES], value[LANES:]
        power = jnp.sum(real * real + imag * imag, axis=1, keepdims=True)
        largest = jnp.max(jnp.maximum(jnp.abs(real), jnp.abs(imag)), axis=1, keepdims=True)
        largest = (largest * np.float32(1.0 + 2.0**-7)).astype(BF16).astype(F32)
        largest = jnp.maximum(largest, np.float32(2.0**-96))
        power_high = power.astype(BF16).astype(F32)
        mine = jnp.where(lane < FIRST, largest, jnp.where(lane < 2 * FIRST, power_high, power - power_high))
        table_scr[...] = jnp.where(lax.rem(lane, FIRST) == c1, mine, table_scr[...])
        scale = SPAN / largest
        for part, piece in enumerate((real, imag)):
            coded = jnp.exp2(piece * scale)
            for c in range(0, LANES, 8):
                channel_scr[part, pl.ds(c * CHANNEL_PITCH + place, 8, stride=CHANNEL_PITCH), :] = coded[c : c + 8]

    def pack(s, h, d):
        for part in range(2):
            for j in range(own):
                start = pl.multiple_of((d * own + j) * CHANNEL_PITCH, 8)
                send_ref[s, h, d, part, j * HALF : (j + 1) * HALF, :] = channel_scr[part, pl.ds(start, HALF), :].astype(BF16)

    blocks = frames // 8

    def one_stream(s, carry):
        load(s).wait()
        lax.fori_loop(2, blocks, lambda tb, c: (transform(s, tb), c)[1], 0)

        @pl.when(me > 0)
        def _():
            pass_on(s).wait_recv()

        lax.fori_loop(0, 2, lambda tb, c: (transform(s, tb), c)[1], 0)
        table_scr[...] = jnp.zeros((LANES, LANES), F32)

        def one_half(h, carry):
            lax.fori_loop(0, HALF, lambda place, c: (second_section(h, place), c)[1], 0)
            lax.fori_loop(0, ways, lambda d, c: (pack(s, h, d), c)[1], 0)
            for number in range(ways - 1):
                outgoing(s, h, number).start()
            own_block(s, h).start()
            return carry

        lax.fori_loop(0, FIRST // HALF, one_half, 0)
        table_ref[s] = table_scr[...].astype(BF16)
        for number in range(ways - 1):
            outgoing_table(s, number).start()
        own_table(s).start()
        return carry

    lax.fori_loop(0, streams, one_stream, 0)

    @pl.when(me < ways - 1)
    def _():
        for s in range(streams):
            pass_on(s).wait_send()

    def finish(s, carry):
        for h in range(FIRST // HALF):
            for number in range(ways - 1):
                outgoing(s, h, number).wait_send()
                incoming(s, h, number).wait_recv()
            own_block(s, h).wait()
        for number in range(ways - 1):
            outgoing_table(s, number).wait_send()
            incoming_table(s, number).wait_recv()
        own_table(s).wait()
        return carry

    lax.fori_loop(0, streams, finish, 0)


def equalize(frames, ways, group, got_ref, scales_ref, out_ref, factor_scr):
    own = LANES // ways

    @pl.when(pl.program_id(1) == 0)
    def _():
        table = scales_ref[0].reshape(ways * own, LANES).astype(F32).T
        largest, power = table[:FIRST], table[FIRST : 2 * FIRST] + table[2 * FIRST : 3 * FIRST]
        step = LANES // 2
        while step >= own:
            power = power + pltpu.roll(power, step, 1)
            step //= 2
        mean = power * np.float32(1.0 / (frames * ways))
        factor_scr[...] = largest * np.float32(math.log2(math.e) / SPAN) * lax.rsqrt(mean + 1.0)

    first = pl.program_id(1) * group
    factors = pltpu.roll(factor_scr[...], lax.rem(LANES - first, LANES), 1)
    for j in range(group):
        for way in range(ways):
            for h in range(FIRST // HALF):
                factor = factors[h * HALF : (h + 1) * HALF, way * own + j : way * own + j + 1]
                for part in range(2):
                    coded = got_ref[0, h, way, part, j * HALF : (j + 1) * HALF, :].astype(F32)
                    row = j * FIRST + h * HALF
                    out_ref[0, part, row : row + HALF, way * LANES : (way + 1) * LANES] = jnp.log(coded) * factor


def shards(signal, taps):
    streams, _, samples = signal.shape
    channels = taps.shape[1]
    ways = lax.axis_size("tm")
    frames = samples // channels
    rows = 2 * FIRST
    own = LANES // ways
    z = signal.reshape(streams, 2, samples // LANES, LANES).transpose(0, 2, 1, 3).reshape(streams, frames * rows, LANES)
    table = section_table()
    high = table.astype(jnp.bfloat16)
    low = (table - high.astype(np.float32)).astype(jnp.bfloat16)
    cos, sin = twist_tables()
    vmem = pl.BlockSpec(memory_space=pltpu.VMEM)
    hbm = pl.BlockSpec(memory_space=pltpu.HBM)
    halves = FIRST // HALF
    dma = pltpu.SemaphoreType.DMA
    got, scales = pl.pallas_call(
        lambda *refs: channelize(streams, frames, ways, *refs),
        out_shape=(
            jax.ShapeDtypeStruct((streams, halves, ways, 2, own * HALF, LANES), BF16),
            jax.ShapeDtypeStruct((streams, ways, own, LANES), BF16),
        ),
        in_specs=[hbm, vmem, vmem, vmem, vmem, vmem],
        out_specs=(hbm, hbm),
        scratch_shapes=[
            pltpu.VMEM((streams, (frames + 16) * rows, LANES), BF16),
            pltpu.VMEM((16 * TAPS_PITCH, LANES), F32),
            pltpu.VMEM((8 * FRAME_PITCH, LANES), F32),
            pltpu.VMEM((FIRST, frames, 2 * LANES), F32),
            pltpu.VMEM((2, LANES * CHANNEL_PITCH, LANES), F32),
            pltpu.VMEM((streams, halves, ways, 2, own * HALF, LANES), BF16),
            pltpu.VMEM((LANES, LANES), F32),
            pltpu.VMEM((streams, LANES, LANES), BF16),
            dma((streams,)),
            dma((streams,)),
            dma((streams,)),
            dma((streams, halves, ways)),
            dma((streams, halves, ways)),
            dma((streams, ways)),
            dma((streams, ways)),
            dma((streams, halves)),
            dma((streams,)),
        ],
        compiler_params=pltpu.CompilerParams(collective_id=0, has_side_effects=True, vmem_limit_bytes=48 << 20),
        name="channelize",
    )(z, taps, jnp.asarray(high), jnp.asarray(low), jnp.asarray(cos), jnp.asarray(sin))
    group = 4
    return pl.pallas_call(
        lambda *refs: equalize(frames, ways, group, *refs),
        grid=(streams, own // group),
        out_shape=jax.ShapeDtypeStruct((streams, 2, channels // ways, frames * ways), F32),
        in_specs=[
            pl.BlockSpec((1, halves, ways, 2, group * HALF, LANES), lambda s, j: (s, 0, 0, 0, j, 0)),
            pl.BlockSpec((1, ways, own, LANES), lambda s, j: (s, 0, 0, 0)),
        ],
        out_specs=pl.BlockSpec((1, 2, group * FIRST, frames * ways), lambda s, j: (s, 0, j, 0)),
        scratch_shapes=[pltpu.VMEM((FIRST, LANES), F32)],
        compiler_params=pltpu.CompilerParams(dimension_semantics=("arbitrary", "arbitrary")),
        name="equalize",
    )(got, scales)


def solution(mesh):
    in_specs = (P("stream", None, "tm"), P())
    out_specs = P("stream", None, "tm", None)
    return jax.shard_map(shards, mesh=mesh, in_specs=in_specs, out_specs=out_specs, check_vma=False)
```

profile of v0, /device:TPU:32, one launch (start us, length us, event | category | flops | bytes accessed | tf_op | source)
XLA Modules:
  0.0 81.8 jit_solution(11599565233447535562)
XLA Ops:
  0.0 0.0 copy-start.1
  0.0 0.9 %copy-done.1 = f32[16,4096]{1,0:T(8,128)S(1)} copy-done((f32[16,4096]{1,0:T(8,128)S(1)}, f32[16,4096]{1,0:T(8,128)}, u32[]{:S(2)}) %copy-start.1) | copy-done | bytes 262168
  1.0 0.0 copy-start.2
  1.0 0.9 %copy-done.2 = bf16[256,256]{1,0:T(8,128)(2,1)S(1)} copy-done((bf16[256,256]{1,0:T(8,128)(2,1)S(1)}, bf16[256,256]{1,0:T(8,128)(2,1)}, u32[]{:S(2)}) %copy-start.2) | copy-done | bytes 131096
  1.9 0.0 copy-start.3
  1.9 0.9 %copy-done.3 = bf16[256,256]{1,0:T(8,128)(2,1)S(1)} copy-done((bf16[256,256]{1,0:T(8,128)(2,1)S(1)}, bf16[256,256]{1,0:T(8,128)(2,1)}, u32[]{:S(2)}) %copy-start.3) | copy-done | bytes 131096
  2.8 0.0 copy-start.5
  2.8 0.7 copy-done.5
  3.5 0.0 copy-start.6
  3.5 0.7 copy-done.6
  4.2 66.1 %channelize.1 = (bf16[2,2,8,2,256,128]{5,4,3,2,1,0:T(8,128)(2,1)S(1)}, bf16[2,8,16,128]{3,2,1,0:T(8,128)(2,1)S(1)}) custom-call(bf16[2,8192,128]{2,1,0:T(8,128)(2,1)} %bitcast.5, f32[16,4096]{1,0:T(8,128)S(1)} %copy-done.1, bf16[256,256]{1,0:T(8,128)(2,1)S(1)} %copy-done.3, bf16[256,256]{1,0:T(8,128)(2,1)S(1)} %copy-done.2, f32[32,128]{1,0:T(8,128)S(1)} %copy-done.6, ...), custom_call_target="tpu_custom_call" | custom-call | tf_op jit(solution)/shard_map/channelize/pallas_call | solution.py:344
  70.3 0.0 copy-start
  70.4 1.9 %copy-done = bf16[2,2,8,2,256,128]{5,4,3,2,1,0:T(8,128)(2,1)} copy-done((bf16[2,2,8,2,256,128]{5,4,3,2,1,0:T(8,128)(2,1)}, bf16[2,2,8,2,256,128]{5,4,3,2,1,0:T(8,128)(2,1)S(1)}, u32[]{:S(2)}) %copy-start) | copy-done | bytes 4194328
  72.3 0.0 copy-start.4
  72.3 0.6 copy-done.4
  72.9 8.9 %equalize.1 = f32[2,2,512,1024]{3,2,1,0:T(8,128)} custom-call(bf16[2,2,8,2,256,128]{5,4,3,2,1,0:T(8,128)(2,1)} %copy-done, bf16[2,8,16,128]{3,2,1,0:T(8,128)(2,1)} %copy-done.4), custom_call_target="tpu_custom_call" | custom-call | tf_op jit(solution)/shard_map/equalize/pallas_call | solution.py:375
Async XLA Ops:
  0.0 0.9 %copy-start.1 = (f32[16,4096]{1,0:T(8,128)S(1)}, f32[16,4096]{1,0:T(8,128)}, u32[]{:S(2)}) copy-start(f32[16,4096]{1,0:T(8,128)} %refs_1_.1) | copy-start | bytes 786436
  1.0 0.9 %copy-start.2 = (bf16[256,256]{1,0:T(8,128)(2,1)S(1)}, bf16[256,256]{1,0:T(8,128)(2,1)}, u32[]{:S(2)}) copy-start(bf16[256,256]{1,0:T(8,128)(2,1)} %constant.9.clone.refs_3_) | copy-start | bytes 393220
  1.9 0.9 %copy-start.3 = (bf16[256,256]{1,0:T(8,128)(2,1)S(1)}, bf16[256,256]{1,0:T(8,128)(2,1)}, u32[]{:S(2)}) copy-start(bf16[256,256]{1,0:T(8,128)(2,1)} %constant.8.clone.refs_2_) | copy-start | bytes 393220
  2.8 0.7 copy-start.5
  3.5 0.7 copy-start.6
  70.3 1.9 %copy-start = (bf16[2,2,8,2,256,128]{5,4,3,2,1,0:T(8,128)(2,1)}, bf16[2,2,8,2,256,128]{5,4,3,2,1,0:T(8,128)(2,1)S(1)}, u32[]{:S(2)}) copy-start(bf16[2,2,8,2,256,128]{5,4,3,2,1,0:T(8,128)(2,1)S(1)} %get-tuple-element.7.refs_0_) | copy-start | bytes 12582916
  72.3 0.6 copy-start.4
where the time goes:
time: 83.1 us; the launch traced here: 81.8 us
  Pallas kernels  75.1 us (90%)
  local copies, waits for them, and re-layouts  6.74 us (8%)
    pallas_call x1, Pallas kernels, shards(): pl.pallas_call(lambda *refs: channelize(streams, frames, ways, *refs), ou...  66.1 us
    pallas_call x1, Pallas kernels, shards(): pl.pallas_call(lambda *refs: equalize(frames, ways, group, *refs), grid=(...  8.94 us
    unnamed x14, local copies, waits for them, and re-layouts  6.74 us

commit v1 on v0

--- a/solution.py
+++ b/solution.py
@@ -14,24 +14,23 @@
 
 LANES = 128
 FIRST = 32
-HALF = 16
+GROUP = 8
 TAPS_PITCH = 72
 FRAME_PITCH = 72
-CHANNEL_PITCH = 24
+UNROLL = 4
+PART_ROWS = 4
 SPAN = 125.0
 PEERS = ((2, 1), (2, 0), (1, 1), (3, 1), (0, 1), (1, 0), (3, 0))
 
 
-def section_table():
+def constant_table():
     index = np.arange(LANES)
     angle = 2.0 * math.pi * (np.outer(index, index) % LANES) / LANES
     cos, sin = np.cos(angle) / 64.0, np.sin(angle) / 64.0
-    return np.block([[cos, sin], [-sin, cos]]).astype(np.float32)
-
-
-def twist_tables():
-    angle = 2.0 * math.pi * np.outer(np.arange(FIRST), np.arange(LANES)) / (FIRST * LANES)
-    return np.cos(angle).astype(np.float32), np.sin(angle).astype(np.float32)
+    matrix = np.block([[cos, sin], [-sin, cos]])
+    high = matrix.astype(jnp.bfloat16).astype(np.float64)
+    twist = 2.0 * math.pi * np.outer(np.arange(FIRST), index) / (FIRST * LANES)
+    return np.concatenate([high, matrix - high, np.concatenate([np.cos(twist), np.sin(twist)], axis=1)]).astype(np.float32)
 
 
 def plus(a, b):
@@ -94,9 +93,9 @@
     return lax.dot_general(a, b, (((1,), (1,)), ((), ())), preferred_element_type=F32)
 
 
-def channelize(streams, frames, ways, z_ref, taps_ref, high_ref, low_ref, cos_ref, sin_ref, got_ref, scales_ref,
-               x_ref, taps_scr, frame_scr, grid_scr, channel_scr, send_ref, table_scr, table_ref,
-               load_sem, halo_send, halo_recv, send_sem, recv_sem, table_send, table_recv, own_sem, own_table_sem):
+def channelize(streams, frames, ways, z_ref, taps_in, constants_in, got_ref, scales_ref,
+               taps_ref, constants_ref, matrix_ref, x_ref, taps_scr, frame_scr, grid_scr, channel_scr, send_ref, table_scr, table_ref,
+               table_load, load_sem, halo_send, halo_recv, send_sem, recv_sem, table_send, table_recv, own_sem, own_table_sem):
     rows = 2 * FIRST
     halo = 16 * rows
     edge = 15 * rows
@@ -125,8 +124,14 @@
             device_id_type=MESH,
         )
 
+    tables = [
+        pltpu.make_async_copy(taps_in, taps_ref, table_load.at[0]),
+        pltpu.make_async_copy(constants_in, constants_ref, table_load.at[1]),
+    ]
+    tables[0].start()
     for s in range(streams):
         load(s).start()
+    tables[1].start()
     pl.semaphore_wait(barrier, ways - 1)
 
     @pl.when(me < ways - 1)
@@ -139,6 +144,10 @@
         for s in range(streams):
             x_ref[s, pl.ds(halo - edge, edge), :] = jnp.zeros((edge, LANES), BF16)
 
+    for copy in tables:
+        copy.wait()
+    for row in range(0, 4 * LANES, 64):
+        matrix_ref[row : row + 64, :] = constants_ref[row : row + 64, :].astype(BF16)
     for octet in range(2):
         for m1 in range(FIRST):
             block = taps_ref[pl.ds(8 * octet, 8), pl.ds(LANES * m1, LANES)]
@@ -146,6 +155,7 @@
                 taps_scr[pl.ds(8 * octet * TAPS_PITCH + 2 * m1 + part, 8, stride=TAPS_PITCH), :] = block
 
     lane = lax.broadcasted_iota(jnp.int32, (LANES, LANES), 1)
+    lane_c1 = lax.bitwise_and(lane, FIRST - 1)
 
     def transform(s, tb):
         for g in range(rows // 16):
@@ -166,7 +176,7 @@
 
         at = pl.ds(pl.multiple_of(8 * tb, 8), 8)
         for c1, (real, imag) in enumerate(first_section(fetch)):
-            cos, sin = cos_ref[c1 : c1 + 1, :], sin_ref[c1 : c1 + 1, :]
+            cos, sin = (constants_ref[4 * LANES + c1 : 4 * LANES + c1 + 1, k * LANES : (k + 1) * LANES] for k in range(2))
             grid_scr[c1, at, 0:LANES] = real * cos + imag * sin
             grid_scr[c1, at, LANES : 2 * LANES] = imag * cos - real * sin
 
@@ -223,12 +233,12 @@
         )
 
     def second_section(h, place):
-        c1 = h * HALF + place
+        c1 = h * GROUP + place
         y = grid_scr[c1]
         high = y.astype(BF16)
         low = (y - high.astype(F32)).astype(BF16)
-        wide = transposed_dot(high_ref[...], jnp.concatenate([high, low], axis=0))
-        value = wide[:, :LANES] + wide[:, LANES:] + transposed_dot(low_ref[...], high)
+        wide = transposed_dot(matrix_ref[: 2 * LANES], jnp.concatenate([high, low], axis=0))
+        value = wide[:, :LANES] + wide[:, LANES:] + transposed_dot(matrix_ref[2 * LANES :], high)
         real, imag = value[:LANES], value[LANES:]
         power = jnp.sum(real * real + imag * imag, axis=1, keepdims=True)
         largest = jnp.max(jnp.maximum(jnp.abs(real), jnp.abs(imag)), axis=1, keepdims=True)
@@ -236,18 +246,18 @@
         largest = jnp.maximum(largest, np.float32(2.0**-96))
         power_high = power.astype(BF16).astype(F32)
         mine = jnp.where(lane < FIRST, largest, jnp.where(lane < 2 * FIRST, power_high, power - power_high))
-        table_scr[...] = jnp.where(lax.rem(lane, FIRST) == c1, mine, table_scr[...])
+        table_scr[...] = jnp.where(lane_c1 == c1, mine, table_scr[...])
         scale = SPAN / largest
         for part, piece in enumerate((real, imag)):
             coded = jnp.exp2(piece * scale)
             for c in range(0, LANES, 8):
-                channel_scr[part, pl.ds(c * CHANNEL_PITCH + place, 8, stride=CHANNEL_PITCH), :] = coded[c : c + 8]
+                channel_scr[part, pl.ds(c * GROUP + place, 8, stride=GROUP), :] = coded[c : c + 8]
 
     def pack(s, h, d):
         for part in range(2):
-            for j in range(own):
-                start = pl.multiple_of((d * own + j) * CHANNEL_PITCH, 8)
-                send_ref[s, h, d, part, j * HALF : (j + 1) * HALF, :] = channel_scr[part, pl.ds(start, HALF), :].astype(BF16)
+            for row in range(0, own * GROUP, 16):
+                start = pl.multiple_of(d * own * GROUP + row, 16)
+                send_ref[s, h, d, part, row : row + 16, :] = channel_scr[part, pl.ds(start, 16), :].astype(BF16)
 
     blocks = frames // 8
 
@@ -262,15 +272,15 @@
         lax.fori_loop(0, 2, lambda tb, c: (transform(s, tb), c)[1], 0)
         table_scr[...] = jnp.zeros((LANES, LANES), F32)
 
-        def one_half(h, carry):
-            lax.fori_loop(0, HALF, lambda place, c: (second_section(h, place), c)[1], 0)
+        def one_group(h, carry):
+            lax.fori_loop(0, GROUP, lambda place, c: (second_section(h, place), c)[1], 0, unroll=UNROLL)
             lax.fori_loop(0, ways, lambda d, c: (pack(s, h, d), c)[1], 0)
             for number in range(ways - 1):
                 outgoing(s, h, number).start()
             own_block(s, h).start()
             return carry
 
-        lax.fori_loop(0, FIRST // HALF, one_half, 0)
+        lax.fori_loop(0, FIRST // GROUP, one_group, 0)
         table_ref[s] = table_scr[...].astype(BF16)
         for number in range(ways - 1):
             outgoing_table(s, number).start()
@@ -285,7 +295,7 @@
             pass_on(s).wait_send()
 
     def finish(s, carry):
-        for h in range(FIRST // HALF):
+        for h in range(FIRST // GROUP):
             for number in range(ways - 1):
                 outgoing(s, h, number).wait_send()
                 incoming(s, h, number).wait_recv()
@@ -299,30 +309,47 @@
     lax.fori_loop(0, streams, finish, 0)
 
 
-def equalize(frames, ways, group, got_ref, scales_ref, out_ref, factor_scr):
+def equalize(streams, frames, ways, part_rows, got_ref, scales_ref, out_ref, factor_scr, out_scr, sem):
     own = LANES // ways
-
-    @pl.when(pl.program_id(1) == 0)
-    def _():
-        table = scales_ref[0].reshape(ways * own, LANES).astype(F32).T
+    parts = own // part_rows
+    for s in range(streams):
+        table = scales_ref[s].reshape(ways * own, LANES).astype(F32).T
         largest, power = table[:FIRST], table[FIRST : 2 * FIRST] + table[2 * FIRST : 3 * FIRST]
         step = LANES // 2
         while step >= own:
             power = power + pltpu.roll(power, step, 1)
             step //= 2
         mean = power * np.float32(1.0 / (frames * ways))
-        factor_scr[...] = largest * np.float32(math.log2(math.e) / SPAN) * lax.rsqrt(mean + 1.0)
-
-    first = pl.program_id(1) * group
-    factors = pltpu.roll(factor_scr[...], lax.rem(LANES - first, LANES), 1)
-    for j in range(group):
+        factor_scr[s] = largest * np.float32(math.log2(math.e) / SPAN) * lax.rsqrt(mean + 1.0)
+
+    def copy_out(s, n):
+        rows = pl.ds(pl.multiple_of(n * part_rows * FIRST, part_rows * FIRST), part_rows * FIRST)
+        return pltpu.make_async_copy(out_scr.at[s, :, rows, :], out_ref.at[s, :, rows, :], sem.at[s, n])
+
+    def one_part(index, carry):
+        s, n = index // parts, lax.rem(index, parts)
+        first = n * part_rows
+        factors = pltpu.roll(factor_scr[s], lax.rem(LANES - first, LANES), 1)
         for way in range(ways):
-            for h in range(FIRST // HALF):
-                factor = factors[h * HALF : (h + 1) * HALF, way * own + j : way * own + j + 1]
-                for part in range(2):
-                    coded = got_ref[0, h, way, part, j * HALF : (j + 1) * HALF, :].astype(F32)
-                    row = j * FIRST + h * HALF
-                    out_ref[0, part, row : row + HALF, way * LANES : (way + 1) * LANES] = jnp.log(coded) * factor
+            for h in range(FIRST // GROUP):
+                for j in range(0, part_rows, 2):
+                    factor = [
+                        factors[h * GROUP : (h + 1) * GROUP, way * own + i : way * own + i + 1] for i in (j, j + 1)
+                    ]
+                    for part in range(2):
+                        start = pl.multiple_of((first + j) * GROUP, 16)
+                        value = jnp.log(got_ref[s, h, way, part, pl.ds(start, 16), :].astype(F32))
+                        for i in range(2):
+                            row = pl.multiple_of((first + j + i) * FIRST + h * GROUP, GROUP)
+                            piece = value[i * GROUP : (i + 1) * GROUP] * factor[i]
+                            out_scr[s, part, pl.ds(row, GROUP), way * LANES : (way + 1) * LANES] = piece
+        copy_out(s, n).start()
+        return carry
+
+    lax.fori_loop(0, streams * parts, one_part, 0)
+    for s in range(streams):
+        for n in range(parts):
+            copy_out(s, n).wait()
 
 
 def shards(signal, taps):
@@ -333,56 +360,58 @@
     rows = 2 * FIRST
     own = LANES // ways
     z = signal.reshape(streams, 2, samples // LANES, LANES).transpose(0, 2, 1, 3).reshape(streams, frames * rows, LANES)
-    table = section_table()
-    high = table.astype(jnp.bfloat16)
-    low = (table - high.astype(np.float32)).astype(jnp.bfloat16)
-    cos, sin = twist_tables()
+    constants = constant_table()
     vmem = pl.BlockSpec(memory_space=pltpu.VMEM)
     hbm = pl.BlockSpec(memory_space=pltpu.HBM)
-    halves = FIRST // HALF
+    groups = FIRST // GROUP
     dma = pltpu.SemaphoreType.DMA
     got, scales = pl.pallas_call(
         lambda *refs: channelize(streams, frames, ways, *refs),
         out_shape=(
-            jax.ShapeDtypeStruct((streams, halves, ways, 2, own * HALF, LANES), BF16),
+            jax.ShapeDtypeStruct((streams, groups, ways, 2, own * GROUP, LANES), BF16),
             jax.ShapeDtypeStruct((streams, ways, own, LANES), BF16),
         ),
-        in_specs=[hbm, vmem, vmem, vmem, vmem, vmem],
-        out_specs=(hbm, hbm),
+        in_specs=[hbm] * 3,
+        out_specs=(vmem, vmem),
         scratch_shapes=[
+            pltpu.VMEM(taps.shape, F32),
+            pltpu.VMEM(constants.shape, F32),
+            pltpu.VMEM((4 * LANES, 2 * LANES), BF16),
             pltpu.VMEM((streams, (frames + 16) * rows, LANES), BF16),
             pltpu.VMEM((16 * TAPS_PITCH, LANES), F32),
             pltpu.VMEM((8 * FRAME_PITCH, LANES), F32),
             pltpu.VMEM((FIRST, frames, 2 * LANES), F32),
-            pltpu.VMEM((2, LANES * CHANNEL_PITCH, LANES), F32),
-            pltpu.VMEM((streams, halves, ways, 2, own * HALF, LANES), BF16),
+            pltpu.VMEM((2, LANES * GROUP, LANES), F32),
+            pltpu.VMEM((streams, groups, ways, 2, own * GROUP, LANES), BF16),
             pltpu.VMEM((LANES, LANES), F32),
             pltpu.VMEM((streams, LANES, LANES), BF16),
+            dma((2,)),
             dma((streams,)),
             dma((streams,)),
             dma((streams,)),
-            dma((streams, halves, ways)),
-            dma((streams, halves, ways)),
+            dma((streams, groups, ways)),
+            dma((streams, groups, ways)),
             dma((streams, ways)),
             dma((streams, ways)),
-            dma((streams, halves)),
+            dma((streams, groups)),
             dma((streams,)),
         ],
         compiler_params=pltpu.CompilerParams(collective_id=0, has_side_effects=True, vmem_limit_bytes=48 << 20),
         name="channelize",
-    )(z, taps, jnp.asarray(high), jnp.asarray(low), jnp.asarray(cos), jnp.asarray(sin))
-    group = 4
+    )(z, taps, jnp.asarray(constants))
+    part_rows = PART_ROWS
+    out_shape = (streams, 2, channels // ways, frames * ways)
     return pl.pallas_call(
-        lambda *refs: equalize(frames, ways, group, *refs),
-        grid=(streams, own // group),
-        out_shape=jax.ShapeDtypeStruct((streams, 2, channels // ways, frames * ways), F32),
-        in_specs=[
-            pl.BlockSpec((1, halves, ways, 2, group * HALF, LANES), lambda s, j: (s, 0, 0, 0, j, 0)),
-            pl.BlockSpec((1, ways, own, LANES), lambda s, j: (s, 0, 0, 0)),
+        lambda *refs: equalize(streams, frames, ways, part_rows, *refs),
+        out_shape=jax.ShapeDtypeStruct(out_shape, F32),
+        in_specs=[vmem, vmem],
+        out_specs=hbm,
+        scratch_shapes=[
+            pltpu.VMEM((streams, FIRST, LANES), F32),
+            pltpu.VMEM(out_shape, F32),
+            dma((streams, own // part_rows)),
         ],
-        out_specs=pl.BlockSpec((1, 2, group * FIRST, frames * ways), lambda s, j: (s, 0, j, 0)),
-        scratch_shapes=[pltpu.VMEM((FIRST, LANES), F32)],
-        compiler_params=pltpu.CompilerParams(dimension_semantics=("arbitrary", "arbitrary")),
+        compiler_params=pltpu.CompilerParams(vmem_limit_bytes=24 << 20),
         name="equalize",
     )(got, scales)
 

time: 83.1 us -> 70.2 us (0.84); the launches traced: 81.8 us -> 69.8 us
  Pallas kernels: 75.1 us -> 67.8 us
  local copies, waits for them, and re-layouts: 6.74 us -> 2 us
    unnamed x14 -> x4, local copies, waits for them, and re-layouts: 6.74 us -> 2 us
    pallas_call x1, Pallas kernels: 8.94 us -> 4.26 us  [shards(): pl.pallas_call(lambda *refs: equalize(streams, frames, ways, part_rows, *...]
    pallas_call x1, Pallas kernels: 66.1 us -> 63.5 us  [shards(): pl.pallas_call(lambda *refs: channelize(streams, frames, ways, *refs), ou...]
where the time goes in v1:
time: 70.2 us; the launch traced here: 69.8 us
  Pallas kernels  67.8 us (97%)
  local copies, waits for them, and re-layouts  2 us (3%)
    pallas_call x1, Pallas kernels, shards(): pl.pallas_call(lambda *refs: channelize(streams, frames, ways, *refs), ou...  63.5 us
    pallas_call x1, Pallas kernels, shards(): pl.pallas_call(lambda *refs: equalize(streams, frames, ways, part_rows, *...  4.26 us
    unnamed x4, local copies, waits for them, and re-layouts  2 us

profile of v1, /device:TPU:32, one launch (start us, length us, event | category | flops | bytes accessed | tf_op | source)
XLA Modules:
  0.0 69.8 jit_solution(16394786136557051139)
XLA Ops:
  0.0 0.0 copy-start
  0.0 1.1 %copy-done = f32[544,256]{1,0:T(8,128)S(1)} copy-done((f32[544,256]{1,0:T(8,128)S(1)}, f32[544,256]{1,0:T(8,128)}, u32[]{:S(2)}) %copy-start) | copy-done | bytes 557080
  1.1 0.0 copy-start.1
  1.1 0.9 %copy-done.1 = f32[16,4096]{1,0:T(8,128)S(1)} copy-done((f32[16,4096]{1,0:T(8,128)S(1)}, f32[16,4096]{1,0:T(8,128)}, u32[]{:S(2)}) %copy-start.1) | copy-done | bytes 262168
  2.0 63.5 %channelize.1 = (bf16[2,4,8,2,128,128]{5,4,3,2,1,0:T(8,128)(2,1)S(1)}, bf16[2,8,16,128]{3,2,1,0:T(8,128)(2,1)S(1)}) custom-call(bf16[2,8192,128]{2,1,0:T(8,128)(2,1)} %bitcast.5, f32[16,4096]{1,0:T(8,128)S(1)} %copy-done.1, f32[544,256]{1,0:T(8,128)S(1)} %copy-done), custom_call_target="tpu_custom_call" | custom-call | tf_op jit(solution)/shard_map/channelize/pallas_call | solution.py:368
  65.5 4.3 %equalize.1 = f32[2,2,512,1024]{3,2,1,0:T(8,128)} custom-call(bf16[2,4,8,2,128,128]{5,4,3,2,1,0:T(8,128)(2,1)S(1)} %get-tuple-element.7.refs_0_, bf16[2,8,16,128]{3,2,1,0:T(8,128)(2,1)S(1)} %get-tuple-element.8.refs_1_), custom_call_target="tpu_custom_call" | custom-call | tf_op jit(solution)/shard_map/equalize/pallas_call | solution.py:404
Async XLA Ops:
  0.0 1.1 %copy-start = (f32[544,256]{1,0:T(8,128)S(1)}, f32[544,256]{1,0:T(8,128)}, u32[]{:S(2)}) copy-start(f32[544,256]{1,0:T(8,128)} %constant.2.clone.refs_2_) | copy-start | bytes 1671172
  1.1 0.9 %copy-start.1 = (f32[16,4096]{1,0:T(8,128)S(1)}, f32[16,4096]{1,0:T(8,128)}, u32[]{:S(2)}) copy-start(f32[16,4096]{1,0:T(8,128)} %refs_1_.1) | copy-start | bytes 786436

commit v2 on v1

--- a/solution.py
+++ b/solution.py
@@ -18,7 +18,7 @@
 TAPS_PITCH = 72
 FRAME_PITCH = 72
 UNROLL = 4
-PART_ROWS = 4
+PART_ROWS = 2
 SPAN = 125.0
 PEERS = ((2, 1), (2, 0), (1, 1), (3, 1), (0, 1), (1, 0), (3, 0))
 
@@ -132,17 +132,17 @@
     for s in range(streams):
         load(s).start()
     tables[1].start()
+    @pl.when(me == 0)
+    def _():
+        for s in range(streams):
+            x_ref[s, pl.ds(halo - edge, edge), :] = jnp.zeros((edge, LANES), BF16)
+
     pl.semaphore_wait(barrier, ways - 1)
 
     @pl.when(me < ways - 1)
     def _():
         for s in range(streams):
             pass_on(s).start()
-
-    @pl.when(me == 0)
-    def _():
-        for s in range(streams):
-            x_ref[s, pl.ds(halo - edge, edge), :] = jnp.zeros((edge, LANES), BF16)
 
     for copy in tables:
         copy.wait()
@@ -323,30 +323,28 @@
         factor_scr[s] = largest * np.float32(math.log2(math.e) / SPAN) * lax.rsqrt(mean + 1.0)
 
     def copy_out(s, n):
-        rows = pl.ds(pl.multiple_of(n * part_rows * FIRST, part_rows * FIRST), part_rows * FIRST)
+        rows = pl.ds(n * part_rows * FIRST, part_rows * FIRST)
         return pltpu.make_async_copy(out_scr.at[s, :, rows, :], out_ref.at[s, :, rows, :], sem.at[s, n])
 
-    def one_part(index, carry):
-        s, n = index // parts, lax.rem(index, parts)
-        first = n * part_rows
-        factors = pltpu.roll(factor_scr[s], lax.rem(LANES - first, LANES), 1)
-        for way in range(ways):
-            for h in range(FIRST // GROUP):
-                for j in range(0, part_rows, 2):
-                    factor = [
-                        factors[h * GROUP : (h + 1) * GROUP, way * own + i : way * own + i + 1] for i in (j, j + 1)
-                    ]
-                    for part in range(2):
-                        start = pl.multiple_of((first + j) * GROUP, 16)
-                        value = jnp.log(got_ref[s, h, way, part, pl.ds(start, 16), :].astype(F32))
-                        for i in range(2):
-                            row = pl.multiple_of((first + j + i) * FIRST + h * GROUP, GROUP)
-                            piece = value[i * GROUP : (i + 1) * GROUP] * factor[i]
-                            out_scr[s, part, pl.ds(row, GROUP), way * LANES : (way + 1) * LANES] = piece
-        copy_out(s, n).start()
+    def one_stream(s, carry):
+        factors = factor_scr[s]
+        for n in range(parts):
+            for way in range(ways):
+                for h in range(FIRST // GROUP):
+                    for j in range(n * part_rows, (n + 1) * part_rows, 2):
+                        factor = [
+                            factors[h * GROUP : (h + 1) * GROUP, way * own + i : way * own + i + 1] for i in (j, j + 1)
+                        ]
+                        for part in range(2):
+                            value = jnp.log(got_ref[s, h, way, part, j * GROUP : (j + 2) * GROUP, :].astype(F32))
+                            for i in range(2):
+                                row = (j + i) * FIRST + h * GROUP
+                                piece = value[i * GROUP : (i + 1) * GROUP] * factor[i]
+                                out_scr[s, part, row : row + GROUP, way * LANES : (way + 1) * LANES] = piece
+            copy_out(s, n).start()
         return carry
 
-    lax.fori_loop(0, streams * parts, one_part, 0)
+    lax.fori_loop(0, streams, one_stream, 0)
     for s in range(streams):
         for n in range(parts):
             copy_out(s, n).wait()
@@ -363,6 +361,7 @@
     constants = constant_table()
     vmem = pl.BlockSpec(memory_space=pltpu.VMEM)
     hbm = pl.BlockSpec(memory_space=pltpu.HBM)
+    stay = pltpu.with_memory_space_constraint
     groups = FIRST // GROUP
     dma = pltpu.SemaphoreType.DMA
     got, scales = pl.pallas_call(
@@ -398,7 +397,7 @@
         ],
         compiler_params=pltpu.CompilerParams(collective_id=0, has_side_effects=True, vmem_limit_bytes=48 << 20),
         name="channelize",
-    )(z, taps, jnp.asarray(constants))
+    )(z, stay(taps, pltpu.HBM), stay(jnp.asarray(constants), pltpu.HBM))
     part_rows = PART_ROWS
     out_shape = (streams, 2, channels // ways, frames * ways)
     return pl.pallas_call(

time: 70.2 us -> 67.5 us (0.962)
  local copies, waits for them, and re-layouts: 2 us -> 0 us
    unnamed x4 -> x0, local copies, waits for them, and re-layouts: 2 us -> none
where the time goes in v2:
time: 67.5 us; the launch traced here: 67.4 us
  Pallas kernels  67.4 us (100%)
    pallas_call x1, Pallas kernels, shards(): pl.pallas_call(lambda *refs: channelize(streams, frames, ways, *refs), ou...  63.5 us
    pallas_call x1, Pallas kernels, shards(): pl.pallas_call(lambda *refs: equalize(streams, frames, ways, part_rows, *...  3.91 us

profile of v2, /device:TPU:32, one launch (start us, length us, event | category | flops | bytes accessed | tf_op | source)
XLA Modules:
  0.0 67.4 jit_solution(9459977560658751887)
XLA Ops:
  0.0 63.5 %channelize.1 = (bf16[2,4,8,2,128,128]{5,4,3,2,1,0:T(8,128)(2,1)S(1)}, bf16[2,8,16,128]{3,2,1,0:T(8,128)(2,1)S(1)}) custom-call(bf16[2,8192,128]{2,1,0:T(8,128)(2,1)} %bitcast.5, f32[16,4096]{1,0:T(8,128)} %refs_1_.1, f32[544,256]{1,0:T(8,128)} %constant.2.clone.refs_2_), custom_call_target="tpu_custom_call" | custom-call | tf_op jit(solution)/shard_map/channelize/pallas_call | solution.py:367
  63.5 3.9 %equalize.1 = f32[2,2,512,1024]{3,2,1,0:T(8,128)} custom-call(bf16[2,4,8,2,128,128]{5,4,3,2,1,0:T(8,128)(2,1)S(1)} %get-tuple-element.7.refs_0_, bf16[2,8,16,128]{3,2,1,0:T(8,128)(2,1)S(1)} %get-tuple-element.8.refs_1_), custom_call_target="tpu_custom_call" | custom-call | tf_op jit(solution)/shard_map/equalize/pallas_call | solution.py:403

commit v3 on v2

--- a/solution.py
+++ b/solution.py
@@ -14,12 +14,15 @@
 
 LANES = 128
 FIRST = 32
-GROUP = 8
+GROUP = 16
 TAPS_PITCH = 72
 FRAME_PITCH = 72
 UNROLL = 4
 PART_ROWS = 2
 SPAN = 125.0
+POWER_SPAN = SPAN / 4.5
+POWER_MID = 4.0
+LOG2_E = math.log2(math.e)
 PEERS = ((2, 1), (2, 0), (1, 1), (3, 1), (0, 1), (1, 0), (3, 0))
 
 
@@ -93,7 +96,7 @@
     return lax.dot_general(a, b, (((1,), (1,)), ((), ())), preferred_element_type=F32)
 
 
-def channelize(streams, frames, ways, z_ref, taps_in, constants_in, got_ref, scales_ref,
+def channelize(streams, frames, ways, z_ref, taps_in, constants_in, got_ref, scales_ref, early_ref,
                taps_ref, constants_ref, matrix_ref, x_ref, taps_scr, frame_scr, grid_scr, channel_scr, send_ref, table_scr, table_ref,
                table_load, load_sem, halo_send, halo_recv, send_sem, recv_sem, table_send, table_recv, own_sem, own_table_sem):
     rows = 2 * FIRST
@@ -155,7 +158,6 @@
                 taps_scr[pl.ds(8 * octet * TAPS_PITCH + 2 * m1 + part, 8, stride=TAPS_PITCH), :] = block
 
     lane = lax.broadcasted_iota(jnp.int32, (LANES, LANES), 1)
-    lane_c1 = lax.bitwise_and(lane, FIRST - 1)
 
     def transform(s, tb):
         for g in range(rows // 16):
@@ -191,13 +193,13 @@
             device_id_type=MESH,
         )
 
-    def outgoing_table(s, number):
+    def outgoing_table(number):
         peer = peer_of(number)
         return pltpu.make_async_remote_copy(
-            src_ref=table_ref.at[s, pl.ds(pl.multiple_of(peer * own, own), own), :],
-            dst_ref=scales_ref.at[s, me],
-            send_sem=table_send.at[s, number],
-            recv_sem=table_recv.at[s, me],
+            src_ref=table_ref.at[pl.ds(pl.multiple_of(peer * own, own), own), :],
+            dst_ref=scales_ref.at[me],
+            send_sem=table_send.at[number],
+            recv_sem=table_recv.at[me],
             device_id={"tm": peer},
             device_id_type=MESH,
         )
@@ -205,9 +207,9 @@
     def own_block(s, h):
         return pltpu.make_async_copy(send_ref.at[s, h, me], got_ref.at[s, h, me], own_sem.at[s, h])
 
-    def own_table(s):
+    def own_table():
         return pltpu.make_async_copy(
-            table_ref.at[s, pl.ds(pl.multiple_of(me * own, own), own), :], scales_ref.at[s, me], own_table_sem.at[s]
+            table_ref.at[pl.ds(pl.multiple_of(me * own, own), own), :], scales_ref.at[me], own_table_sem.at[0]
         )
 
     def incoming(s, h, number):
@@ -221,18 +223,18 @@
             device_id_type=MESH,
         )
 
-    def incoming_table(s, number):
+    def incoming_table(number):
         peer = peer_of(number)
         return pltpu.make_async_remote_copy(
-            src_ref=table_ref.at[s, pl.ds(pl.multiple_of(peer * own, own), own), :],
-            dst_ref=scales_ref.at[s, peer],
-            send_sem=table_send.at[s, number],
-            recv_sem=table_recv.at[s, peer],
+            src_ref=table_ref.at[pl.ds(pl.multiple_of(peer * own, own), own), :],
+            dst_ref=scales_ref.at[peer],
+            send_sem=table_send.at[number],
+            recv_sem=table_recv.at[peer],
             device_id={"tm": peer},
             device_id_type=MESH,
         )
 
-    def second_section(h, place):
+    def second_section(s, h, place):
         c1 = h * GROUP + place
         y = grid_scr[c1]
         high = y.astype(BF16)
@@ -244,10 +246,12 @@
         largest = jnp.max(jnp.maximum(jnp.abs(real), jnp.abs(imag)), axis=1, keepdims=True)
         largest = (largest * np.float32(1.0 + 2.0**-7)).astype(BF16).astype(F32)
         largest = jnp.maximum(largest, np.float32(2.0**-96))
-        power_high = power.astype(BF16).astype(F32)
-        mine = jnp.where(lane < FIRST, largest, jnp.where(lane < 2 * FIRST, power_high, power - power_high))
-        table_scr[...] = jnp.where(lane_c1 == c1, mine, table_scr[...])
-        scale = SPAN / largest
+        inverse = 1.0 / largest
+        scale = inverse * SPAN
+        ratio = jnp.log(power * inverse * inverse) * np.float32(POWER_SPAN * LOG2_E) - np.float32(POWER_SPAN * POWER_MID)
+        place_in_table = 2 * FIRST * s + c1
+        table = jnp.where(lane == place_in_table, largest, table_scr[...])
+        table_scr[...] = jnp.where(lane == place_in_table + FIRST, jnp.exp2(ratio), table)
         for part, piece in enumerate((real, imag)):
             coded = jnp.exp2(piece * scale)
             for c in range(0, LANES, 8):
@@ -260,6 +264,8 @@
                 send_ref[s, h, d, part, row : row + 16, :] = channel_scr[part, pl.ds(start, 16), :].astype(BF16)
 
     blocks = frames // 8
+    groups = FIRST // GROUP
+    table_scr[...] = jnp.zeros((LANES, LANES), F32)
 
     def one_stream(s, carry):
         load(s).wait()
@@ -270,21 +276,24 @@
             pass_on(s).wait_recv()
 
         lax.fori_loop(0, 2, lambda tb, c: (transform(s, tb), c)[1], 0)
-        table_scr[...] = jnp.zeros((LANES, LANES), F32)
 
         def one_group(h, carry):
-            lax.fori_loop(0, GROUP, lambda place, c: (second_section(h, place), c)[1], 0, unroll=UNROLL)
+            lax.fori_loop(0, GROUP, lambda place, c: (second_section(s, h, place), c)[1], 0, unroll=UNROLL)
+
+            @pl.when(s * groups + h == streams * groups - 1)
+            def _():
+                table_ref[...] = table_scr[...].astype(BF16)
+                for number in range(ways - 1):
+                    outgoing_table(number).start()
+                own_table().start()
+
             lax.fori_loop(0, ways, lambda d, c: (pack(s, h, d), c)[1], 0)
             for number in range(ways - 1):
                 outgoing(s, h, number).start()
             own_block(s, h).start()
             return carry
 
-        lax.fori_loop(0, FIRST // GROUP, one_group, 0)
-        table_ref[s] = table_scr[...].astype(BF16)
-        for number in range(ways - 1):
-            outgoing_table(s, number).start()
-        own_table(s).start()
+        lax.fori_loop(0, groups, one_group, 0)
         return carry
 
     lax.fori_loop(0, streams, one_stream, 0)
@@ -294,57 +303,76 @@
         for s in range(streams):
             pass_on(s).wait_send()
 
-    def finish(s, carry):
+    for number in range(ways - 1):
+        outgoing_table(number).wait_send()
+        incoming_table(number).wait_recv()
+    own_table().wait()
+    for s in range(streams):
         for h in range(FIRST // GROUP):
             for number in range(ways - 1):
                 outgoing(s, h, number).wait_send()
                 incoming(s, h, number).wait_recv()
             own_block(s, h).wait()
-        for number in range(ways - 1):
-            outgoing_table(s, number).wait_send()
-            incoming_table(s, number).wait_recv()
-        own_table(s).wait()
-        return carry
-
-    lax.fori_loop(0, streams, finish, 0)
-
-
-def equalize(streams, frames, ways, part_rows, got_ref, scales_ref, out_ref, factor_scr, out_scr, sem):
+        if s < streams - 1:
+            factors = factors_of(frames, scales_ref[...], s)
+
+            def decode_part(n, factors, s=s):
+                for j in range(0, PART_ROWS, 2):
+                    decode_rows(ways, got_ref.at[s], early_ref.at[s], n * PART_ROWS + j, j, factors)
+                return pltpu.roll(factors, LANES - PART_ROWS, 1)
+
+            lax.fori_loop(0, own // PART_ROWS, decode_part, factors)
+
+
+def factors_of(frames, scales, s):
+    ways, own, _ = scales.shape
+    table = scales.reshape(ways * own, LANES).astype(F32).T
+    largest, ratio = table[2 * FIRST * s : 2 * FIRST * s + FIRST], table[2 * FIRST * s + FIRST : 2 * FIRST * (s + 1)]
+    ratio = jnp.exp2(jnp.log(ratio) * np.float32(LOG2_E / POWER_SPAN) + np.float32(POWER_MID))
+    power = largest * largest * ratio
+    step = LANES // 2
+    while step >= own:
+        power = power + pltpu.roll(power, step, 1)
+        step //= 2
+    mean = power * np.float32(1.0 / (frames * ways))
+    return largest * np.float32(LOG2_E / SPAN) * lax.rsqrt(mean + 1.0)
+
+
+def decode_rows(ways, got, out, first, column, factors):
     own = LANES // ways
-    parts = own // part_rows
-    for s in range(streams):
-        table = scales_ref[s].reshape(ways * own, LANES).astype(F32).T
-        largest, power = table[:FIRST], table[FIRST : 2 * FIRST] + table[2 * FIRST : 3 * FIRST]
-        step = LANES // 2
-        while step >= own:
-            power = power + pltpu.roll(power, step, 1)
-            step //= 2
-        mean = power * np.float32(1.0 / (frames * ways))
-        factor_scr[s] = largest * np.float32(math.log2(math.e) / SPAN) * lax.rsqrt(mean + 1.0)
+    for way in range(ways):
+        for h in range(FIRST // GROUP):
+            for part in range(2):
+                start = first * GROUP
+                start = start if isinstance(start, int) else pl.multiple_of(start, 2 * GROUP)
+                value = jnp.log(got[h, way, part, pl.ds(start, 2 * GROUP), :].astype(F32))
+                for i in range(2):
+                    at = way * own + column + i
+                    row = (first + i) * FIRST + h * GROUP
+                    row = row if isinstance(row, int) else pl.multiple_of(row, GROUP)
+                    piece = value[i * GROUP : (i + 1) * GROUP] * factors[h * GROUP : (h + 1) * GROUP, at : at + 1]
+                    out[part, pl.ds(row, GROUP), way * LANES : (way + 1) * LANES] = piece
+
+
+def equalize(streams, frames, ways, got_ref, scales_ref, early_ref, out_ref, late_ref, sem):
+    own = LANES // ways
+    last = streams - 1
+    size = PART_ROWS * FIRST
 
     def copy_out(s, n):
-        rows = pl.ds(n * part_rows * FIRST, part_rows * FIRST)
-        return pltpu.make_async_copy(out_scr.at[s, :, rows, :], out_ref.at[s, :, rows, :], sem.at[s, n])
-
-    def one_stream(s, carry):
-        factors = factor_scr[s]
+        source = early_ref.at[s] if s < last else late_ref
+        rows = pl.ds(n * size, size)
+        return pltpu.make_async_copy(source.at[:, rows, :], out_ref.at[s, :, rows, :], sem.at[s, n])
+
+    parts = own // PART_ROWS
+    for s in range(last):
         for n in range(parts):
-            for way in range(ways):
-                for h in range(FIRST // GROUP):
-                    for j in range(n * part_rows, (n + 1) * part_rows, 2):
-                        factor = [
-                            factors[h * GROUP : (h + 1) * GROUP, way * own + i : way * own + i + 1] for i in (j, j + 1)
-                        ]
-                        for part in range(2):
-                            value = jnp.log(got_ref[s, h, way, part, j * GROUP : (j + 2) * GROUP, :].astype(F32))
-                            for i in range(2):
-                                row = (j + i) * FIRST + h * GROUP
-                                piece = value[i * GROUP : (i + 1) * GROUP] * factor[i]
-                                out_scr[s, part, row : row + GROUP, way * LANES : (way + 1) * LANES] = piece
             copy_out(s, n).start()
-        return carry
-
-    lax.fori_loop(0, streams, one_stream, 0)
+    factors = factors_of(frames, scales_ref[...], last)
+    for n in range(parts):
+        for j in range(n * PART_ROWS, (n + 1) * PART_ROWS, 2):
+            decode_rows(ways, got_ref.at[last], late_ref, j, j, factors)
+        copy_out(last, n).start()
     for s in range(streams):
         for n in range(parts):
             copy_out(s, n).wait()
@@ -364,14 +392,16 @@
     stay = pltpu.with_memory_space_constraint
     groups = FIRST // GROUP
     dma = pltpu.SemaphoreType.DMA
-    got, scales = pl.pallas_call(
+    share = channels // ways
+    got, scales, early = pl.pallas_call(
         lambda *refs: channelize(streams, frames, ways, *refs),
         out_shape=(
             jax.ShapeDtypeStruct((streams, groups, ways, 2, own * GROUP, LANES), BF16),
-            jax.ShapeDtypeStruct((streams, ways, own, LANES), BF16),
+            jax.ShapeDtypeStruct((ways, own, LANES), BF16),
+            jax.ShapeDtypeStruct((streams - 1, 2, share, frames * ways), F32),
         ),
         in_specs=[hbm] * 3,
-        out_specs=(vmem, vmem),
+        out_specs=(vmem, vmem, vmem),
         scratch_shapes=[
             pltpu.VMEM(taps.shape, F32),
             pltpu.VMEM(constants.shape, F32),
@@ -383,36 +413,30 @@
             pltpu.VMEM((2, LANES * GROUP, LANES), F32),
             pltpu.VMEM((streams, groups, ways, 2, own * GROUP, LANES), BF16),
             pltpu.VMEM((LANES, LANES), F32),
-            pltpu.VMEM((streams, LANES, LANES), BF16),
+            pltpu.VMEM((LANES, LANES), BF16),
             dma((2,)),
             dma((streams,)),
             dma((streams,)),
             dma((streams,)),
             dma((streams, groups, ways)),
             dma((streams, groups, ways)),
-            dma((streams, ways)),
-            dma((streams, ways)),
+            dma((ways,)),
+            dma((ways,)),
             dma((streams, groups)),
-            dma((streams,)),
+            dma((1,)),
         ],
-        compiler_params=pltpu.CompilerParams(collective_id=0, has_side_effects=True, vmem_limit_bytes=48 << 20),
+        compiler_params=pltpu.CompilerParams(collective_id=0, has_side_effects=True, vmem_limit_bytes=40 << 20),
         name="channelize",
-    )(z, stay(taps, pltpu.HBM), stay(jnp.asarray(constants), pltpu.HBM))
-    part_rows = PART_ROWS
-    out_shape = (streams, 2, channels // ways, frames * ways)
+    )(stay(z, pltpu.HBM), stay(taps, pltpu.HBM), stay(jnp.asarray(constants), pltpu.HBM))
     return pl.pallas_call(
-        lambda *refs: equalize(streams, frames, ways, part_rows, *refs),
-        out_shape=jax.ShapeDtypeStruct(out_shape, F32),
-        in_specs=[vmem, vmem],
+        lambda *refs: equalize(streams, frames, ways, *refs),
+        out_shape=jax.ShapeDtypeStruct((streams, 2, share, frames * ways), F32),
+        in_specs=[vmem, vmem, vmem],
         out_specs=hbm,
-        scratch_shapes=[
-            pltpu.VMEM((streams, FIRST, LANES), F32),
-            pltpu.VMEM(out_shape, F32),
-            dma((streams, own // part_rows)),
-        ],
+        scratch_shapes=[pltpu.VMEM((2, share, frames * ways), F32), dma((streams, own // PART_ROWS))],
         compiler_params=pltpu.CompilerParams(vmem_limit_bytes=24 << 20),
         name="equalize",
-    )(got, scales)
+    )(got, scales, early)
 
 
 def solution(mesh):

time: 67.5 us -> 66 us (0.978)
  Pallas kernels: 67.4 us -> 65.7 us
    pallas_call x1, Pallas kernels: 63.5 us -> 62.1 us  [shards(): pl.pallas_call(lambda *refs: channelize(streams, frames, ways, *refs), ou...]
where the time goes in v3:
time: 66 us; the launch traced here: 65.7 us
  Pallas kernels  65.7 us (100%)
    pallas_call x1, Pallas kernels, shards(): pl.pallas_call(lambda *refs: channelize(streams, frames, ways, *refs), ou...  62.1 us
    pallas_call x1, Pallas kernels, shards(): pl.pallas_call(lambda *refs: equalize(streams, frames, ways, *refs), out_...  3.6 us

profile of v3, /device:TPU:32, one launch (start us, length us, event | category | flops | bytes accessed | tf_op | source)
XLA Modules:
  0.0 65.7 jit_solution(12484879170725583373)
XLA Ops:
  0.0 62.1 %channelize.1 = (bf16[2,2,8,2,256,128]{5,4,3,2,1,0:T(8,128)(2,1)S(1)}, bf16[8,16,128]{2,1,0:T(8,128)(2,1)S(1)}, f32[1,2,512,1024]{3,2,1,0:T(8,128)S(1)}) custom-call(bf16[2,8192,128]{2,1,0:T(8,128)(2,1)} %bitcast.5, f32[16,4096]{1,0:T(8,128)} %refs_1_.1, f32[544,256]{1,0:T(8,128)} %constant.2.clone.refs_2_), custom_call_target="tpu_custom_call" | custom-call | tf_op jit(solution)/shard_map/channelize/pallas_call | solution.py:396
  62.1 3.6 %equalize.1 = f32[2,2,512,1024]{3,2,1,0:T(8,128)} custom-call(bf16[2,2,8,2,256,128]{5,4,3,2,1,0:T(8,128)(2,1)S(1)} %get-tuple-element.8.refs_0_, bf16[8,16,128]{2,1,0:T(8,128)(2,1)S(1)} %get-tuple-element.9.refs_1_, f32[1,2,512,1024]{3,2,1,0:T(8,128)S(1)} %get-tuple-element.10.refs_2_), custom_call_target="tpu_custom_call" | custom-call | tf_op jit(solution)/shard_map/equalize/pallas_call | solution.py:431

commit v4 on v3

--- a/solution.py
+++ b/solution.py
@@ -17,8 +17,8 @@
 GROUP = 16
 TAPS_PITCH = 72
 FRAME_PITCH = 72
-UNROLL = 4
-PART_ROWS = 2
+UNROLL = 8
+PART_ROWS = 4
 SPAN = 125.0
 POWER_SPAN = SPAN / 4.5
 POWER_MID = 4.0
@@ -96,8 +96,8 @@
     return lax.dot_general(a, b, (((1,), (1,)), ((), ())), preferred_element_type=F32)
 
 
-def channelize(streams, frames, ways, z_ref, taps_in, constants_in, got_ref, scales_ref, early_ref,
-               taps_ref, constants_ref, matrix_ref, x_ref, taps_scr, frame_scr, grid_scr, channel_scr, send_ref, table_scr, table_ref,
+def channelize(streams, frames, ways, z_ref, taps_in, constants_in, got_ref, factors_ref, early_ref, late_ref,
+               scales_ref, taps_ref, constants_ref, matrix_ref, x_ref, taps_scr, frame_scr, grid_scr, channel_scr, send_ref, table_scr, table_ref,
                table_load, load_sem, halo_send, halo_recv, send_sem, recv_sem, table_send, table_recv, own_sem, own_table_sem):
     rows = 2 * FIRST
     halo = 16 * rows
@@ -245,7 +245,7 @@
         power = jnp.sum(real * real + imag * imag, axis=1, keepdims=True)
         largest = jnp.max(jnp.maximum(jnp.abs(real), jnp.abs(imag)), axis=1, keepdims=True)
         largest = (largest * np.float32(1.0 + 2.0**-7)).astype(BF16).astype(F32)
-        largest = jnp.maximum(largest, np.float32(2.0**-96))
+        largest = jnp.maximum(largest, np.float32(2.0**-118))
         inverse = 1.0 / largest
         scale = inverse * SPAN
         ratio = jnp.log(power * inverse * inverse) * np.float32(POWER_SPAN * LOG2_E) - np.float32(POWER_SPAN * POWER_MID)
@@ -307,18 +307,22 @@
         outgoing_table(number).wait_send()
         incoming_table(number).wait_recv()
     own_table().wait()
+    scales = scales_ref[...]
+    factors_ref[...] = factors_of(frames, scales, streams - 1)
     for s in range(streams):
-        for h in range(FIRST // GROUP):
+        factors = factors_of(frames, scales, s)
+        for h in range(groups):
             for number in range(ways - 1):
                 outgoing(s, h, number).wait_send()
                 incoming(s, h, number).wait_recv()
             own_block(s, h).wait()
-        if s < streams - 1:
-            factors = factors_of(frames, scales_ref[...], s)
-
-            def decode_part(n, factors, s=s):
-                for j in range(0, PART_ROWS, 2):
-                    decode_rows(ways, got_ref.at[s], early_ref.at[s], n * PART_ROWS + j, j, factors)
+            if (s, h) == (streams - 1, groups - 1):
+                break
+            target = early_ref.at[s] if s < streams - 1 else late_ref
+
+            def decode_part(n, factors, s=s, h=h, target=target):
+                for j in range(PART_ROWS):
+                    decode_row(ways, got_ref.at[s, h], target, n * PART_ROWS + j, j, h * GROUP, factors[h * GROUP : (h + 1) * GROUP])
                 return pltpu.roll(factors, LANES - PART_ROWS, 1)
 
             lax.fori_loop(0, own // PART_ROWS, decode_part, factors)
@@ -338,44 +342,46 @@
     return largest * np.float32(LOG2_E / SPAN) * lax.rsqrt(mean + 1.0)
 
 
-def decode_rows(ways, got, out, first, column, factors):
+def decode_row(ways, got, out, j, column, row, factors):
     own = LANES // ways
+    start = j * GROUP
+    start = start if isinstance(start, int) else pl.multiple_of(start, GROUP)
     for way in range(ways):
-        for h in range(FIRST // GROUP):
-            for part in range(2):
-                start = first * GROUP
-                start = start if isinstance(start, int) else pl.multiple_of(start, 2 * GROUP)
-                value = jnp.log(got[h, way, part, pl.ds(start, 2 * GROUP), :].astype(F32))
-                for i in range(2):
-                    at = way * own + column + i
-                    row = (first + i) * FIRST + h * GROUP
-                    row = row if isinstance(row, int) else pl.multiple_of(row, GROUP)
-                    piece = value[i * GROUP : (i + 1) * GROUP] * factors[h * GROUP : (h + 1) * GROUP, at : at + 1]
-                    out[part, pl.ds(row, GROUP), way * LANES : (way + 1) * LANES] = piece
-
-
-def equalize(streams, frames, ways, got_ref, scales_ref, early_ref, out_ref, late_ref, sem):
+        at = way * own + column
+        for part in range(2):
+            value = jnp.log(got[way, part, pl.ds(start, GROUP), :].astype(F32))
+            out[part, j, row : row + GROUP, way * LANES : (way + 1) * LANES] = value * factors[:, at : at + 1]
+
+
+def equalize(streams, ways, got_ref, factors_ref, early_ref, late_ref, out_ref, last_ref, early_sem, late_sem, last_sem):
     own = LANES // ways
-    last = streams - 1
-    size = PART_ROWS * FIRST
-
-    def copy_out(s, n):
-        source = early_ref.at[s] if s < last else late_ref
-        rows = pl.ds(n * size, size)
-        return pltpu.make_async_copy(source.at[:, rows, :], out_ref.at[s, :, rows, :], sem.at[s, n])
-
-    parts = own // PART_ROWS
-    for s in range(last):
-        for n in range(parts):
-            copy_out(s, n).start()
-    factors = factors_of(frames, scales_ref[...], last)
-    for n in range(parts):
-        for j in range(n * PART_ROWS, (n + 1) * PART_ROWS, 2):
-            decode_rows(ways, got_ref.at[last], late_ref, j, j, factors)
-        copy_out(last, n).start()
-    for s in range(streams):
-        for n in range(parts):
-            copy_out(s, n).wait()
+    s, h = streams - 1, FIRST // GROUP - 1
+
+    def copy_early(n):
+        return pltpu.make_async_copy(early_ref.at[n], out_ref.at[n], early_sem.at[n])
+
+    def copy_late():
+        return pltpu.make_async_copy(late_ref, out_ref.at[s, :, :, pl.ds(0, h * GROUP), :], late_sem.at[0])
+
+    def copy_last(n):
+        rows = pl.ds(n * PART_ROWS, PART_ROWS)
+        return pltpu.make_async_copy(
+            last_ref.at[:, rows], out_ref.at[s, :, rows, pl.ds(h * GROUP, GROUP), :], last_sem.at[n]
+        )
+
+    for n in range(s):
+        copy_early(n).start()
+    copy_late().start()
+    factors = factors_ref[h * GROUP :, :]
+    for n in range(own // PART_ROWS):
+        for j in range(n * PART_ROWS, (n + 1) * PART_ROWS):
+            decode_row(ways, got_ref.at[s, h], last_ref, j, j, 0, factors)
+        copy_last(n).start()
+    for n in range(s):
+        copy_early(n).wait()
+    copy_late().wait()
+    for n in range(own // PART_ROWS):
+        copy_last(n).wait()
 
 
 def shards(signal, taps):
@@ -393,24 +399,26 @@
     groups = FIRST // GROUP
     dma = pltpu.SemaphoreType.DMA
     share = channels // ways
-    got, scales, early = pl.pallas_call(
+    got, factors, early, late = pl.pallas_call(
         lambda *refs: channelize(streams, frames, ways, *refs),
         out_shape=(
             jax.ShapeDtypeStruct((streams, groups, ways, 2, own * GROUP, LANES), BF16),
-            jax.ShapeDtypeStruct((ways, own, LANES), BF16),
-            jax.ShapeDtypeStruct((streams - 1, 2, share, frames * ways), F32),
+            jax.ShapeDtypeStruct((FIRST, LANES), F32),
+            jax.ShapeDtypeStruct((streams - 1, 2, own, FIRST, frames * ways), F32),
+            jax.ShapeDtypeStruct((2, own, FIRST - GROUP, frames * ways), F32),
         ),
         in_specs=[hbm] * 3,
-        out_specs=(vmem, vmem, vmem),
+        out_specs=(vmem, vmem, vmem, vmem),
         scratch_shapes=[
+            pltpu.VMEM((ways, own, LANES), BF16),
             pltpu.VMEM(taps.shape, F32),
             pltpu.VMEM(constants.shape, F32),
             pltpu.VMEM((4 * LANES, 2 * LANES), BF16),
             pltpu.VMEM((streams, (frames + 16) * rows, LANES), BF16),
-            pltpu.VMEM((16 * TAPS_PITCH, LANES), F32),
-            pltpu.VMEM((8 * FRAME_PITCH, LANES), F32),
+            pltpu.VMEM((17 * TAPS_PITCH, LANES), F32),
+            pltpu.VMEM((9 * FRAME_PITCH, LANES), F32),
             pltpu.VMEM((FIRST, frames, 2 * LANES), F32),
-            pltpu.VMEM((2, LANES * GROUP, LANES), F32),
+            pltpu.VMEM((2, (LANES + 1) * GROUP, LANES), F32),
             pltpu.VMEM((streams, groups, ways, 2, own * GROUP, LANES), BF16),
             pltpu.VMEM((LANES, LANES), F32),
             pltpu.VMEM((LANES, LANES), BF16),
@@ -428,15 +436,21 @@
         compiler_params=pltpu.CompilerParams(collective_id=0, has_side_effects=True, vmem_limit_bytes=40 << 20),
         name="channelize",
     )(stay(z, pltpu.HBM), stay(taps, pltpu.HBM), stay(jnp.asarray(constants), pltpu.HBM))
-    return pl.pallas_call(
-        lambda *refs: equalize(streams, frames, ways, *refs),
-        out_shape=jax.ShapeDtypeStruct((streams, 2, share, frames * ways), F32),
-        in_specs=[vmem, vmem, vmem],
+    out = pl.pallas_call(
+        lambda *refs: equalize(streams, ways, *refs),
+        out_shape=jax.ShapeDtypeStruct((streams, 2, own, FIRST, frames * ways), F32),
+        in_specs=[vmem, vmem, vmem, vmem],
         out_specs=hbm,
-        scratch_shapes=[pltpu.VMEM((2, share, frames * ways), F32), dma((streams, own // PART_ROWS))],
-        compiler_params=pltpu.CompilerParams(vmem_limit_bytes=24 << 20),
+        scratch_shapes=[
+            pltpu.VMEM((2, own, GROUP, frames * ways), F32),
+            dma((streams - 1,)),
+            dma((1,)),
+            dma((own // PART_ROWS,)),
+        ],
+        compiler_params=pltpu.CompilerParams(vmem_limit_bytes=16 << 20),
         name="equalize",
-    )(got, scales, early)
+    )(got, factors, early, late)
+    return out.reshape(streams, 2, share, frames * ways)
 
 
 def solution(mesh):

time: 66 us -> 65.4 us (level)
  Pallas kernels: 65.7 us -> 65 us
where the time goes in v4:
time: 65.4 us; the launch traced here: 65 us
  Pallas kernels  65 us (99%)
    pallas_call x1, Pallas kernels, shards(): pl.pallas_call(lambda *refs: channelize(streams, frames, ways, *refs), ou...  61.7 us
    pallas_call x1, Pallas kernels, shards(): pl.pallas_call(lambda *refs: equalize(streams, ways, *refs), out_shape=ja...  3.33 us

profile of v4, /device:TPU:32, one launch (start us, length us, event | category | flops | bytes accessed | tf_op | source)
XLA Modules:
  0.0 65.0 jit_solution(3884532419381868021)
XLA Ops:
  0.0 61.7 %channelize.1 = (bf16[2,2,8,2,256,128]{5,4,3,2,1,0:T(8,128)(2,1)S(1)}, f32[32,128]{1,0:T(8,128)S(1)}, f32[1,2,16,32,1024]{4,3,2,1,0:T(8,128)S(1)}, f32[2,16,16,1024]{3,2,1,0:T(8,128)S(1)}) custom-call(bf16[2,8192,128]{2,1,0:T(8,128)(2,1)} %bitcast.6, f32[16,4096]{1,0:T(8,128)} %refs_1_.1, f32[544,256]{1,0:T(8,128)} %constant.2.clone.refs_2_), custom_call_target="tpu_custom_call" | custom-call | tf_op jit(solution)/shard_map/channelize/pallas_call | solution.py:402
  61.7 3.3 %equalize.1 = f32[2,2,16,32,1024]{4,3,2,1,0:T(8,128)} custom-call(bf16[2,2,8,2,256,128]{5,4,3,2,1,0:T(8,128)(2,1)S(1)} %get-tuple-element.9.refs_0_, f32[32,128]{1,0:T(8,128)S(1)} %get-tuple-element.10.refs_1_, f32[1,2,16,32,1024]{4,3,2,1,0:T(8,128)S(1)} %get-tuple-element.11.refs_2_, f32[2,16,16,1024]{3,2,1,0:T(8,128)S(1)} %get-tuple-element.12.refs_3_), custom_call_target="tpu_custom_call" | custom-call | tf_op jit(solution)/shard_map/equalize/pallas_call | solution.py:439

commit v5 on v4

--- a/solution.py
+++ b/solution.py
@@ -17,7 +17,7 @@
 GROUP = 16
 TAPS_PITCH = 72
 FRAME_PITCH = 72
-UNROLL = 8
+UNROLL = 16
 PART_ROWS = 4
 SPAN = 125.0
 POWER_SPAN = SPAN / 4.5
@@ -159,7 +159,8 @@
 
     lane = lax.broadcasted_iota(jnp.int32, (LANES, LANES), 1)
 
-    def transform(s, tb):
+    def transform(s, tb, slot):
+        base = slot * 9 * FRAME_PITCH
         for g in range(rows // 16):
             total = [None] * 8
             for j in range(23):
@@ -171,10 +172,11 @@
                         term = taps_scr[k * TAPS_PITCH + 16 * g : k * TAPS_PITCH + 16 * g + 16, :] * x
                         total[o] = term if total[o] is None else total[o] + term
             for o in range(8):
-                frame_scr[o * FRAME_PITCH + 16 * g : o * FRAME_PITCH + 16 * g + 16, :] = total[o]
+                start = base + o * FRAME_PITCH + 16 * g
+                frame_scr[start : start + 16, :] = total[o]
 
         def fetch(m1):
-            return tuple(frame_scr[pl.ds(2 * m1 + part, 8, stride=FRAME_PITCH), :] for part in range(2))
+            return tuple(frame_scr[pl.ds(base + 2 * m1 + part, 8, stride=FRAME_PITCH), :] for part in range(2))
 
         at = pl.ds(pl.multiple_of(8 * tb, 8), 8)
         for c1, (real, imag) in enumerate(first_section(fetch)):
@@ -269,13 +271,19 @@
 
     def one_stream(s, carry):
         load(s).wait()
-        lax.fori_loop(2, blocks, lambda tb, c: (transform(s, tb), c)[1], 0)
+
+        def two_blocks(pair, carry):
+            for slot in range(2):
+                transform(s, 2 * pair + slot, slot)
+            return carry
+
+        lax.fori_loop(1, blocks // 2, two_blocks, 0)
 
         @pl.when(me > 0)
         def _():
             pass_on(s).wait_recv()
 
-        lax.fori_loop(0, 2, lambda tb, c: (transform(s, tb), c)[1], 0)
+        lax.fori_loop(0, 1, two_blocks, 0)
 
         def one_group(h, carry):
             lax.fori_loop(0, GROUP, lambda place, c: (second_section(s, h, place), c)[1], 0, unroll=UNROLL)
@@ -416,7 +424,7 @@
             pltpu.VMEM((4 * LANES, 2 * LANES), BF16),
             pltpu.VMEM((streams, (frames + 16) * rows, LANES), BF16),
             pltpu.VMEM((17 * TAPS_PITCH, LANES), F32),
-            pltpu.VMEM((9 * FRAME_PITCH, LANES), F32),
+            pltpu.VMEM((18 * FRAME_PITCH, LANES), F32),
             pltpu.VMEM((FIRST, frames, 2 * LANES), F32),
             pltpu.VMEM((2, (LANES + 1) * GROUP, LANES), F32),
             pltpu.VMEM((streams, groups, ways, 2, own * GROUP, LANES), BF16),

time: 65.4 us -> 66 us (level); the launches traced: 65 us -> 64.7 us
  no operation moved by 1% of the time
where the time goes in v5:
time: 66 us; the launch traced here: 64.7 us
  Pallas kernels  64.7 us (98%)
    pallas_call x1, Pallas kernels, shards(): pl.pallas_call(lambda *refs: channelize(streams, frames, ways, *refs), ou...  61.4 us
    pallas_call x1, Pallas kernels, shards(): pl.pallas_call(lambda *refs: equalize(streams, ways, *refs), out_shape=ja...  3.33 us

profile of v5, /device:TPU:32, one launch (start us, length us, event | category | flops | bytes accessed | tf_op | source)
XLA Modules:
  0.0 64.7 jit_solution(11524860758783323494)
XLA Ops:
  0.0 61.4 %channelize.1 = (bf16[2,2,8,2,256,128]{5,4,3,2,1,0:T(8,128)(2,1)S(1)}, f32[32,128]{1,0:T(8,128)S(1)}, f32[1,2,16,32,1024]{4,3,2,1,0:T(8,128)S(1)}, f32[2,16,16,1024]{3,2,1,0:T(8,128)S(1)}) custom-call(bf16[2,8192,128]{2,1,0:T(8,128)(2,1)} %bitcast.6, f32[16,4096]{1,0:T(8,128)} %refs_1_.1, f32[544,256]{1,0:T(8,128)} %constant.2.clone.refs_2_), custom_call_target="tpu_custom_call" | custom-call | tf_op jit(solution)/shard_map/channelize/pallas_call | solution.py:410
  61.4 3.3 %equalize.1 = f32[2,2,16,32,1024]{4,3,2,1,0:T(8,128)} custom-call(bf16[2,2,8,2,256,128]{5,4,3,2,1,0:T(8,128)(2,1)S(1)} %get-tuple-element.9.refs_0_, f32[32,128]{1,0:T(8,128)S(1)} %get-tuple-element.10.refs_1_, f32[1,2,16,32,1024]{4,3,2,1,0:T(8,128)S(1)} %get-tuple-element.11.refs_2_, f32[2,16,16,1024]{3,2,1,0:T(8,128)S(1)} %get-tuple-element.12.refs_3_), custom_call_target="tpu_custom_call" | custom-call | tf_op jit(solution)/shard_map/equalize/pallas_call | solution.py:447
